TPU v7x, 32 devices: a whole 2x2x4 slice. The times are simulated.
32 devices in a mesh: replica: 4 (over y, core), fsdp: 8 (over z, x).
Axes of the slice: x: 2, y: 2, z: 4, core: 2. Of those that a mesh axis runs over, the one named last changes fastest.
Arguments:
- layer_input: bfloat16 [2, 4096, 4096], P(None, ('replica', 'fsdp')), may hold values from -6 to 6
- queries: bfloat16 [2, 4096, 4096], P(None, ('replica', 'fsdp')), may hold values from -100 to 100
- keys: bfloat16 [2, 4096, 512], P(None, ('replica', 'fsdp')), may hold values from -8 to 8
- targets: bfloat16 [2, 4096, 4096], P(None, ('replica', 'fsdp')), may hold values from -6 to 6
- value_weight: float32 [4096, 512], P('fsdp'), may hold values from -6 to 6
- outer_momentum: float32 [4096, 512], P('fsdp'), may hold values from -0.6 to 0.6
Outputs:
- new_weight: float32 [4096, 512], P('fsdp')
- new_momentum: float32 [4096, 512], P('fsdp')
All inputs are finite; a program needn't handle non-finite values.
Results may differ from a plain program's by a relative error of at most 0.0017.
Values may be sent and summed in bfloat16 or wider, within the bound.
A program may use at most 64 MiB of HBM per device.

v0:
```python
import math

import jax
import jax.numpy as jnp
from jax import lax
from jax.sharding import PartitionSpec as P

D = 4096
QH = 32
KVH = 4
HD = 128


beta_one = 0.9
beta_two = 0.95
inner_rate = 0.05
decay_rate = 0.1
outer_rate = 0.7
outer_mu = 0.9


def shards(layer_input, queries, keys, targets, value_weight, outer_momentum):
    inner_steps = layer_input.shape[0]
    length = layer_input.shape[1]
    columns = value_weight.shape[1]
    fsdp_count = lax.axis_size("fsdp")
    replicas = lax.axis_size("replica")
    tok_rep = length * fsdp_count
    group_size = QH // KVH
    adam_floor = math.sqrt(group_size / (tok_rep * D))
    by_features = lax.all_to_all(layer_input, "fsdp", split_axis=2, concat_axis=1, tiled=True)
    causal = jnp.arange(length)[:, None] >= jnp.arange(length)[None, :]
    weights_now = value_weight
    moment_one = jnp.zeros_like(value_weight)
    moment_two = jnp.zeros_like(value_weight)
    for step_index in range(inner_steps):
        inputs = layer_input[step_index]
        shard_bf = weights_now.astype(jnp.bfloat16)
        product = jnp.dot(
            inputs,
            lax.all_gather(shard_bf, "fsdp", axis=0, tiled=True),
            preferred_element_type=jnp.float32,
        )
        values = (product / math.sqrt(D)).astype(jnp.bfloat16)
        query_heads = queries[step_index].reshape(length, KVH, group_size, HD)
        key_heads = keys[step_index].reshape(length, KVH, HD)
        scores = jnp.einsum(
            "qgjd,kgd->gjqk", query_heads, key_heads, preferred_element_type=jnp.float32
        ) / math.sqrt(HD)
        scores = jnp.where(causal, scores, -1e30)
        highest = jnp.max(scores, axis=-1, keepdims=True)
        expd = jnp.exp(scores - highest)
        attention = (expd / jnp.sum(expd, axis=-1, keepdims=True)).astype(jnp.bfloat16)
        attended = jnp.einsum(
            "gjqk,kgd->qgjd",
            attention,
            values.reshape(length, KVH, HD),
            preferred_element_type=jnp.float32,
        ).reshape(length, QH * HD)
        out_grad = ((attended - targets[step_index].astype(jnp.float32)) / tok_rep).astype(
            jnp.bfloat16
        )
        value_grad = (
            jnp.einsum(
                "gjqk,qgjd->kgd",
                attention,
                out_grad.reshape(length, KVH, group_size, HD),
                preferred_element_type=jnp.float32,
            )
            .reshape(length, columns)
            .astype(jnp.bfloat16)
        )
        step_features = by_features[step_index]
        gradient = lax.dot_general(
            step_features,
            lax.all_gather(value_grad, "fsdp", axis=0, tiled=True),
            (((0,), (0,)), ((), ())),
            preferred_element_type=jnp.float32,
        ) / math.sqrt(D)
        moment_one = beta_one * moment_one + (1.0 - beta_one) * gradient
        moment_two = beta_two * moment_two + (1.0 - beta_two) * gradient * gradient
        corrected_one = moment_one / (1.0 - beta_one ** (step_index + 1))
        corrected_two = moment_two / (1.0 - beta_two ** (step_index + 1))
        weights_now = weights_now - inner_rate * (
            corrected_one / (jnp.sqrt(corrected_two) + adam_floor) + decay_rate * weights_now
        )
    total_delta = lax.psum(value_weight - weights_now, "replica")
    mean_delta = total_delta / replicas
    new_momentum = outer_mu * outer_momentum + mean_delta
    new_weight = value_weight - outer_rate * (mean_delta + outer_mu * new_momentum)
    return (new_weight, new_momentum)


def solution(mesh):
    in_specs = (
        P(None, ("replica", "fsdp"), None),
        P(None, ("replica", "fsdp"), None),
        P(None, ("replica", "fsdp"), None),
        P(None, ("replica", "fsdp"), None),
        P("fsdp", None),
        P("fsdp", None),
    )
    out_specs = (P("fsdp", None), P("fsdp", None))
    return jax.shard_map(shards, mesh=mesh, in_specs=in_specs, out_specs=out_specs, check_vma=False)
```

profile of v0, /device:TPU:0, one launch (start us, length us, event | category | flops | bytes accessed | tf_op | source)
XLA Modules:
  0.0 342.8 jit_solution(9082489792045507031)
XLA Ops:
  7.2 2.3 convert_element_type.61
  9.5 3.8 %copy.71 = bf16[2,128,4096]{1,0,2:T(2,128)(2,1)} copy(bf16[2,128,4096]{2,1,0:T(8,128)(2,1)S(1)} %copy-done) | data formatting | bytes 4194304 | tf_op args[0]
  13.3 7.3 %all-to-all-start = ((bf16[2,128,4096]{1,0,2:T(2,128)(2,1)}), bf16[2,128,4096]{1,0,2:T(2,128)(2,1)}, u32[]{:S(2)}, u32[]{:S(2)}) async-start(bf16[2,128,4096]{1,0,2:T(2,128)(2,1)} %copy.71), calls=%async_computation | async-start | bytes 4194304 | tf_op jit(solution)/shard_map/all_to_all | solution.py:31
  20.6 3.4 slice_convert_fusion.1
  24.0 3.0 copy.69
  27.2 2.7 fusion.55
  29.9 1.3 copy.107
  31.2 3.4 fusion.57
  34.6 86.8 %all-gather.5.cloned.1.call-done = bf16[4096,512]{1,0:T(8,128)(2,1)} async-done(((bf16[512,512]{1,0:T(8,128)(2,1)}), bf16[4096,512]{1,0:T(8,128)(2,1)}) %all-gather.5.cloned.1.call-update) | async-done | bytes 4194320 | tf_op jit(solution)/shard_map/all_gather | solution.py:41
  121.4 3.2 fusion.14
  124.7 4.3 %fusion.12 = bf16[4,128,128]{2,1,0:T(8,128)(2,1)} fusion(f32[128,4,8,128]{0,3,2,1:T(8,128)} %bitcast.151, bf16[128,4,128,1]{0,2,3,1:T(8,128)(2,1)S(1)} %bitcast.161, f32[4,8,128,128]{2,3,1,0:T(8,128)} %get-tuple-element.21, f32[4,8,128]{2,1,0:T(8,128)S(1)} %get-tuple-element.20), kind=kOutput, calls=%fused_computation.22 | convolution fusion | flops 272171008 | bytes 4472832 | tf_op jit(solution)/shard_map/gjqk,qgjd->kgd/dot_general | solution.py:64
  129.1 1.6 copy.86
  130.7 1.9 copy.72
  132.5 1.5 fusion.54
  134.0 2.3 copy.73
  136.3 30.1 %all-gather.7.cloned.1.call-done = bf16[1024,512]{0,1:T(8,128)(2,1)} async-done(((bf16[128,512]{0,1:T(8,128)(2,1)}), bf16[1024,512]{0,1:T(8,128)(2,1)}) %all-gather.7.cloned.1.call-update) | async-done | bytes 1048592 | tf_op jit(solution)/shard_map/all_gather | solution.py:76
  166.4 3.9 %fusion.43 = (bf16[512,512]{0,1:T(8,128)(2,1)}, f32[512,512]{1,0:T(8,128)}) fusion(f32[512,512]{0,1:T(8,128)S(1)} %copy.86, bf16[1024,512]{0,1:T(8,128)(2,1)} %all-gather.7.cloned.1.call-done, bf16[1024,512]{1,0:T(8,128)(2,1)} %bitcast.153), kind=kOutput, calls=%fused_computation.58 | convolution fusion | flops 539754496 | bytes 4718592 | tf_op jit(solution)/shard_map/dot_general | solution.py:74
  170.4 1.8 copy.81
  172.4 2.3 copy.109
  174.7 3.5 %fusion.58 = (f32[4,8,128]{2,1,0:T(8,128)S(1)}, f32[4,8,128,128]{2,3,1,0:T(8,128)}) fusion(pred[128,128]{0,1:T(8,128)(4,1)S(1)} %iota_compare_fusion, bf16[128,4,128,1]{0,2,3,1:T(8,128)(2,1)S(1)} %bitcast.160, bf16[128,4,8,128]{0,3,2,1:T(8,128)(2,1)} %bitcast.156), kind=kOutput, calls=%fused_computation.72 | convolution fusion | flops 136315008 | bytes 3309568 | tf_op jit(solution)/shard_map/sub | solution.py:52
  178.2 66.0 %all-gather.9.cloned.1.call-done = bf16[4096,512]{0,1:T(8,128)(2,1)} async-done(((bf16[512,512]{0,1:T(8,128)(2,1)}), bf16[4096,512]{0,1:T(8,128)(2,1)}) %all-gather.9.cloned.1.call-update) | async-done | bytes 4194320 | tf_op jit(solution)/shard_map/all_gather | solution.py:41
  244.2 3.4 %fusion.15 = bf16[512,128]{1,0:T(8,128)(2,1)S(1)} fusion(bf16[4096,512]{0,1:T(8,128)(2,1)} %all-gather.9.cloned.1.call-done, bf16[2,128,4096]{2,1,0:T(8,128)(2,1)S(1)} %copy-done.1), kind=kOutput, calls=%fused_computation.25 | convolution fusion | flops 537001984 | bytes 5373952 | tf_op jit(solution)/shard_map/dot_general | solution.py:39
  247.6 4.4 %fusion.13 = bf16[4,128,128]{2,1,0:T(8,128)(2,1)} fusion(f32[128,4,8,128]{0,3,2,1:T(8,128)} %bitcast.152, bf16[128,4,128,1]{0,2,3,1:T(8,128)(2,1)S(1)} %bitcast.162, f32[4,8,128,128]{2,3,1,0:T(8,128)} %get-tuple-element.25, f32[4,8,128]{2,1,0:T(8,128)S(1)} %get-tuple-element.24), kind=kOutput, calls=%fused_computation.23 | convolution fusion | flops 272171008 | bytes 4472832 | tf_op jit(solution)/shard_map/gjqk,qgjd->kgd/dot_general | solution.py:64
  252.0 0.2 all-reduce.2.cloned.1.call-start
  252.3 0.5 copy.83
  252.8 36.9 %all-gather.11.cloned.1.call-done = bf16[1024,512]{0,1:T(8,128)(2,1)} async-done(((bf16[128,512]{0,1:T(8,128)(2,1)}), bf16[1024,512]{0,1:T(8,128)(2,1)}) %all-gather.11.cloned.1.call-update) | async-done | bytes 1048592 | tf_op jit(solution)/shard_map/all_gather | solution.py:76
  289.8 4.6 %fusion.23 = f32[512,512]{0,1:T(8,128)} fusion(f32[512,512]{0,1:T(8,128)S(1)} %copy.86, f32[512,512]{1,0:T(8,128)} %get-tuple-element.23, bf16[1024,512]{0,1:T(8,128)(2,1)} %all-gather.11.cloned.1.call-done, bf16[1024,512]{1,0:T(8,128)(2,1)S(1)} %bitcast.154), kind=kOutput, calls=%fused_computation.34 | convolution fusion | flops 543948800 | bytes 5242880 | tf_op jit(solution)/shard_map/dot_general | solution.py:74
  294.4 0.3 copy.85
  294.7 35.1 %all-reduce.2.cloned.1.call-done = f32[512,512]{0,1:T(8,128)} async-done(((f32[512,512]{0,1:T(8,128)}), f32[512,512]{0,1:T(8,128)}) %all-reduce.2.cloned.1.call-update) | async-done | bytes 1048592 | tf_op jit(solution)/shard_map/psum | solution.py:87
  329.8 2.6 multiply_add_fusion
  332.4 2.5 copy.87
  335.0 1.3 copy.88
  (25 shorter events, 0.7 us)
Async XLA Ops:
  7.2 2.3 copy-start
  7.2 114.2 %all-gather.5.cloned.1.call-start = ((), (), s32[]{:S(2)}) async-start(), calls=%async_computation.1 | async-start | bytes 4718592 | tf_op jit(solution)/shard_map/all_gather | solution.py:41
  13.3 117.4 %all-to-all-start = ((bf16[2,128,4096]{1,0,2:T(2,128)(2,1)}), bf16[2,128,4096]{1,0,2:T(2,128)(2,1)}, u32[]{:S(2)}, u32[]{:S(2)}) async-start(bf16[2,128,4096]{1,0,2:T(2,128)(2,1)} %copy.71), calls=%async_computation | async-start | bytes 4194304 | tf_op jit(solution)/shard_map/all_to_all | solution.py:31
  20.6 145.9 %all-gather.7.cloned.1.call-start = ((), (), s32[]{:S(2)}) async-start(), calls=%async_computation.2 | async-start | bytes 1179648 | tf_op jit(solution)/shard_map/all_gather | solution.py:76
  24.0 3.0 copy-start.4
  129.1 115.1 %all-gather.9.cloned.1.call-start = ((), (), s32[]{:S(2)}) async-start(), calls=%async_computation.3 | async-start | bytes 4718592 | tf_op jit(solution)/shard_map/all_gather | solution.py:41
  170.4 119.4 %all-gather.11.cloned.1.call-start = ((), (), s32[]{:S(2)}) async-start(), calls=%async_computation.4 | async-start | bytes 1179648 | tf_op jit(solution)/shard_map/all_gather | solution.py:76
  174.7 69.5 %copy-start.1 = (bf16[2,128,4096]{2,1,0:T(8,128)(2,1)S(1)}, bf16[2,128,4096]{2,1,0:T(8,128)(2,1)}, u32[]{:S(2)}) copy-start(bf16[2,128,4096]{2,1,0:T(8,128)(2,1)} %param.6) | copy-start | bytes 6291460
  247.6 4.6 %copy-start.2 = (bf16[1,8,128,512]{2,3,1,0:T(8,128)(2,1)S(1)}, bf16[1,8,128,512]{2,3,1,0:T(8,128)(2,1)}, u32[]{:S(2)}) copy-start(bf16[1,8,128,512]{2,3,1,0:T(8,128)(2,1)} %get-tuple-element.12) | copy-start | bytes 3145732
  252.0 77.8 %all-reduce.2.cloned.1.call-start = ((), (), s32[]{:S(2)}) async-start(), calls=%async_computation.5 | async-start | bytes 2097152 | tf_op jit(solution)/shard_map/psum | solution.py:87
  289.8 4.6 %copy-start.3 = (f32[512,512]{1,0:T(8,128)S(1)}, f32[512,512]{1,0:T(8,128)}, u32[]{:S(2)}) copy-start(f32[512,512]{1,0:T(8,128)} %param.11) | copy-start | bytes 3145732
Sparse Core Ops, SparseCore 0:
  10.1 111.2 all-gather.4
  129.2 37.2 all-gather.6
  170.5 73.6 all-gather.8
  252.1 37.5 all-gather.10
  294.5 35.2 all-reduce.1
where the time goes:
time: 343 us
  waiting for transfers between devices  255 us (74%)
  matrix products  30.8 us (9%)
  local copies, waits for them, and re-layouts  27.2 us (8%)
  between operations  13.9 us (4%)
  other arithmetic  8.29 us (2%)
  starting transfers between devices  7.66 us (2%)
    all_gather x2, waiting for transfers between devices, shards(): lax.all_gather(shard_bf, 'fsdp', axis=0, tiled=True)  153 us
    all_gather x2, waiting for transfers between devices, shards(): lax.all_gather(value_grad, 'fsdp', axis=0, tiled=True)  67.1 us
    psum x1, waiting for transfers between devices, shards(): total_delta = lax.psum(value_weight - weights_now, 'replica')  35.1 us
    unnamed x19, local copies, waits for them, and re-layouts  13.4 us
    dot_general x2, matrix products, shards(): jnp.einsum('gjqk,qgjd->kgd', attention, out_grad.reshape(length, KVH, gro...  8.66 us
    dot_general x2, matrix products, shards(): lax.dot_general(step_features, lax.all_gather(value_grad, 'fsdp', axis=0,...  8.49 us
    all_to_all x1, starting transfers between devices, shards(): lax.all_to_all(layer_input, 'fsdp', split_axis=2, concat_axis=1, tiled=True)  7.28 us
    sub x2, matrix products, shards(): expd = jnp.exp(scores - highest)  6.95 us
  transfers between devices with their start and end apart: 6, of which 5 were waited for; matrix products, arithmetic and copies ran while one was open for 12% of the time, Pallas kernels for 0%

commit v1 on v0

--- a/solution.py
+++ b/solution.py
@@ -1,8 +1,11 @@
+import functools
 import math
 
 import jax
 import jax.numpy as jnp
 from jax import lax
+from jax.experimental import pallas as pl
+from jax.experimental.pallas import tpu as pltpu
 from jax.sharding import PartitionSpec as P
 
 D = 4096
@@ -19,7 +22,7 @@
 outer_mu = 0.9
 
 
-def shards(layer_input, queries, keys, targets, value_weight, outer_momentum):
+def plain_shards(layer_input, queries, keys, targets, value_weight, outer_momentum):
     inner_steps = layer_input.shape[0]
     length = layer_input.shape[1]
     columns = value_weight.shape[1]
@@ -91,6 +94,379 @@
     return (new_weight, new_momentum)
 
 
+MESH = pl.DeviceIdType.MESH
+
+
+def round_kernel(
+    n,
+    x_ref,
+    q_ref,
+    k_ref,
+    t_ref,
+    w_ref,
+    om_ref,
+    nw_ref,
+    nm_ref,
+    feat,
+    mat_hi,
+    mat_lo,
+    base,
+    side_out,
+    side_in,
+    col_out,
+    col_in,
+    vgrad,
+    grad,
+    theta,
+    mom_one,
+    mom_two,
+    wbf,
+    acc,
+    delta,
+    core_in,
+    pair_out,
+    pair_in,
+    total,
+    in_s,
+    in_r,
+    side_s,
+    side_r,
+    col_s,
+    col_r,
+    agz_s,
+    agz_r,
+    agx_s,
+    agx_r,
+    rep_s,
+    rep_r,
+):
+    steps, length, _ = x_ref.shape
+    rows, columns = w_ref.shape
+    heads = columns // HD
+    group = QH // KVH
+    tok_rep = length * n
+    adam_floor = math.sqrt(group / (tok_rep * D))
+    nz = n // 2
+    me = lax.axis_index("fsdp")
+    rep = lax.axis_index("replica")
+    z, px = me // 2, me % 2
+    core = rep % 2
+    core_peer = rep + 1 - 2 * core
+    pair_peer = (rep + 2) % 4
+    side = z * 2 + (1 - px)
+
+    def at(dz, dx):
+        return ((z + dz + nz) % nz) * 2 + (px + dx) % 2
+
+    hops = [(dz, 1) for dz in range(nz)] + [(dz, 0) for dz in range(1, nz)]
+
+    barrier = pltpu.get_barrier_semaphore()
+    for dz, dx in hops:
+        pl.semaphore_signal(barrier, inc=1, device_id={"fsdp": at(dz, dx)}, device_id_type=MESH)
+    for peer in (core_peer, pair_peer):
+        pl.semaphore_signal(barrier, inc=1, device_id={"replica": peer}, device_id_type=MESH)
+    pl.semaphore_wait(barrier, n + 1)
+
+    def send(src, dst, ssem, rsem, axis, peer):
+        copy = pltpu.make_async_remote_copy(
+            src_ref=src,
+            dst_ref=dst,
+            send_sem=ssem,
+            recv_sem=rsem,
+            device_id={axis: peer},
+            device_id_type=MESH,
+        )
+        copy.start()
+        return copy
+
+    def send_inputs(s):
+        copies = {}
+        for dz, dx in hops:
+            peer = at(dz, dx)
+            i = dz * 2 + dx
+            copies[dz, dx] = send(
+                x_ref.at[s, :, pl.ds(pl.multiple_of(peer * rows, 128), rows)],
+                feat.at[s, me],
+                in_s.at[s, i],
+                in_r.at[s, i],
+                "fsdp",
+                peer,
+            )
+        return copies
+
+    causal = lax.broadcasted_iota(jnp.int32, (length, length), 0) >= lax.broadcasted_iota(
+        jnp.int32, (length, length), 1
+    )
+
+    def attention_of(s):
+        def one(g, carry):
+            keys = k_ref[s, :, pl.ds(pl.multiple_of(g * HD, HD), HD)]
+            both = jnp.zeros((length, length + HD), jnp.float32)
+            for j in range(group):
+                cols = pl.ds(pl.multiple_of((g * group + j) * HD, HD), HD)
+                scores = lax.dot_general(
+                    q_ref[s, :, cols],
+                    keys,
+                    (((1,), (1,)), ((), ())),
+                    preferred_element_type=jnp.float32,
+                ) / math.sqrt(HD)
+                scores = jnp.where(causal, scores, -1e30)
+                highest = jnp.max(scores, axis=-1, keepdims=True)
+                expd = jnp.exp(scores - highest)
+                att = (expd / jnp.sum(expd, axis=-1, keepdims=True)).astype(jnp.bfloat16)
+                both += lax.dot_general(
+                    att,
+                    jnp.concatenate([att, t_ref[s, :, cols]], axis=1),
+                    (((0,), (0,)), ((), ())),
+                    preferred_element_type=jnp.float32,
+                )
+            gram = both[:, :length]
+            high = gram.astype(jnp.bfloat16)
+            mat_hi[s, g] = high
+            mat_lo[s, g] = (gram - high.astype(jnp.float32)).astype(jnp.bfloat16)
+            base[s, g] = both[:, length:]
+            return carry
+
+        lax.fori_loop(0, heads, one, 0)
+
+    chunk = 32
+
+    def chunks(body):
+        def step(i, carry):
+            body(pl.ds(pl.multiple_of(i * chunk, chunk), chunk))
+            return carry
+
+        lax.fori_loop(0, rows // chunk, step, 0)
+
+    pending = []
+    inputs = {0: send_inputs(0)}
+    for s in range(steps):
+        feat[s, me] = x_ref[s, :, pl.ds(pl.multiple_of(me * rows, 128), rows)]
+
+    def cast_weights(c):
+        wbf[c, :] = w_ref[c, :].astype(jnp.bfloat16)
+
+    chunks(cast_weights)
+    for s in range(steps):
+        attention_of(s)
+
+    for s in range(steps):
+        def partial(j):
+            return jnp.dot(feat[s, j], wbf[...], preferred_element_type=jnp.float32)
+
+        def wait_input(dz, dx):
+            inputs[s][(nz - dz) % nz, dx].wait_recv()
+
+        sides = []
+        for dz in range(nz):
+            wait_input(dz, 1)
+            side_out[s, dz] = partial(at(dz, 1)).astype(jnp.bfloat16)
+            sides.append(
+                send(
+                    side_out.at[s, dz],
+                    side_in.at[s, dz],
+                    side_s.at[s, dz],
+                    side_r.at[s, dz],
+                    "fsdp",
+                    side,
+                )
+            )
+        cols = []
+        for dz in list(range(1, nz)) + [0]:
+            if dz:
+                wait_input(dz, 0)
+            own = partial(at(dz, 0))
+            sides[dz].wait_recv()
+            own = own + side_in[s, dz].astype(jnp.float32)
+            if dz:
+                col_out[s, dz] = own.astype(jnp.bfloat16)
+                cols.append(
+                    send(
+                        col_out.at[s, dz],
+                        col_in.at[s, dz],
+                        col_s.at[s, dz],
+                        col_r.at[s, dz],
+                        "fsdp",
+                        at(dz, 0),
+                    )
+                )
+            else:
+                acc[...] = own
+        if s + 1 < steps:
+            inputs[s + 1] = send_inputs(s + 1)
+        for dz in range(1, nz):
+            cols[dz - 1].wait_recv()
+        pending += sides + cols + list(inputs[s].values())
+
+        summed = acc[...]
+        for dz in range(1, nz):
+            summed = summed + col_in[s, dz].astype(jnp.float32)
+        values = (summed / math.sqrt(D)).astype(jnp.bfloat16)
+        for g in range(heads):
+            part = values[:, g * HD : (g + 1) * HD]
+            vg = jnp.dot(mat_hi[s, g], part, preferred_element_type=jnp.float32)
+            vg += jnp.dot(mat_lo[s, g], part, preferred_element_type=jnp.float32)
+            vg = (vg - base[s, g]) / tok_rep
+            vgrad[s, me, :, g * HD : (g + 1) * HD] = vg.astype(jnp.bfloat16)
+
+        def add_block(j, first=False):
+            term = lax.dot_general(
+                feat[s, j],
+                vgrad[s, j],
+                (((0,), (0,)), ((), ())),
+                preferred_element_type=jnp.float32,
+            )
+            if first:
+                grad[...] = term
+            else:
+                grad[...] += term
+
+        zs = []
+        for dz in range(1, nz):
+            zs.append(
+                send(
+                    vgrad.at[s, me],
+                    vgrad.at[s, me],
+                    agz_s.at[s, dz],
+                    agz_r.at[s, dz],
+                    "fsdp",
+                    at(dz, 0),
+                )
+            )
+        xs = [
+            send(
+                vgrad.at[s, me], vgrad.at[s, me], agx_s.at[s, 0], agx_r.at[s, 0], "fsdp", side
+            )
+        ]
+        add_block(me, True)
+        for dz in (1, *range(nz - 1, 1, -1)):
+            j = at(-dz, 0)
+            zs[dz - 1].wait_recv()
+            xs.append(
+                send(
+                    vgrad.at[s, j],
+                    vgrad.at[s, j],
+                    agx_s.at[s, dz],
+                    agx_r.at[s, dz],
+                    "fsdp",
+                    side,
+                )
+            )
+            add_block(j)
+        for i, dz in enumerate((0, 1, *range(nz - 1, 1, -1))):
+            xs[i].wait_recv()
+            add_block(at(-dz, 1))
+        pending += zs + xs
+
+        def adam(c):
+            gradient = grad[c, :] / math.sqrt(D)
+            one = (1.0 - beta_one) * gradient
+            two = (1.0 - beta_two) * gradient * gradient
+            if s:
+                one = beta_one * mom_one[c, :] + one
+                two = beta_two * mom_two[c, :] + two
+            now = theta[c, :] if s else w_ref[c, :]
+            fixed_one = one / (1.0 - beta_one ** (s + 1))
+            fixed_two = two / (1.0 - beta_two ** (s + 1))
+            now = now - inner_rate * (
+                fixed_one / (jnp.sqrt(fixed_two) + adam_floor) + decay_rate * now
+            )
+            if s + 1 < steps:
+                mom_one[c, :] = one
+                mom_two[c, :] = two
+                theta[c, :] = now
+                wbf[c, :] = now.astype(jnp.bfloat16)
+            else:
+                delta[c, :] = w_ref[c, :] - now
+
+        chunks(adam)
+
+    half = rows // 2
+    mine = pl.ds(pl.multiple_of(core * half, 128), half)
+    other = pl.ds(pl.multiple_of((1 - core) * half, 128), half)
+    first = send(delta.at[other], core_in, rep_s.at[0], rep_r.at[0], "replica", core_peer)
+    first.wait_recv()
+    pair_out[...] = (delta[mine, :] + core_in[...]).astype(jnp.bfloat16)
+    second = send(pair_out, pair_in, rep_s.at[1], rep_r.at[1], "replica", pair_peer)
+    second.wait_recv()
+    total[mine, :] = pair_out[...].astype(jnp.float32) + pair_in[...].astype(jnp.float32)
+    third = send(
+        total.at[mine], total.at[mine], rep_s.at[2], rep_r.at[2], "replica", core_peer
+    )
+
+    def finish(start):
+        def step(i, carry):
+            c = pl.ds(pl.multiple_of(start + i * chunk, chunk), chunk)
+            mean = total[c, :] / 4
+            momentum = outer_mu * om_ref[c, :] + mean
+            nm_ref[c, :] = momentum
+            nw_ref[c, :] = w_ref[c, :] - outer_rate * (mean + outer_mu * momentum)
+            return carry
+
+        lax.fori_loop(0, half // chunk, step, 0)
+
+    finish(core * half)
+    third.wait_recv()
+    finish((1 - core) * half)
+    for copy in pending + [first, second, third]:
+        copy.wait_send()
+
+
+def shards(layer_input, queries, keys, targets, value_weight, outer_momentum):
+    n = lax.axis_size("fsdp")
+    replicas = lax.axis_size("replica")
+    rows, columns = value_weight.shape
+    steps, length, _ = layer_input.shape
+    if rows % 256 or n % 2 or replicas != 4 or length % 128:
+        return plain_shards(layer_input, queries, keys, targets, value_weight, outer_momentum)
+    nz = n // 2
+    heads = columns // HD
+    bf, f32 = jnp.bfloat16, jnp.float32
+    dma = pltpu.SemaphoreType.DMA
+    out = jax.ShapeDtypeStruct((rows, columns), f32)
+    return pl.pallas_call(
+        functools.partial(round_kernel, n),
+        out_shape=(out, out),
+        in_specs=[pl.BlockSpec(memory_space=pltpu.VMEM)] * 6,
+        out_specs=(pl.BlockSpec(memory_space=pltpu.VMEM),) * 2,
+        scratch_shapes=[
+            pltpu.VMEM((steps, n, length, rows), bf),
+            pltpu.VMEM((steps, heads, length, length), bf),
+            pltpu.VMEM((steps, heads, length, length), bf),
+            pltpu.VMEM((steps, heads, length, HD), f32),
+            pltpu.VMEM((steps, nz, length, columns), bf),
+            pltpu.VMEM((steps, nz, length, columns), bf),
+            pltpu.VMEM((steps, nz, length, columns), bf),
+            pltpu.VMEM((steps, nz, length, columns), bf),
+            pltpu.VMEM((steps, n, length, columns), bf),
+            pltpu.VMEM((rows, columns), f32),
+            pltpu.VMEM((rows, columns), f32),
+            pltpu.VMEM((rows, columns), f32),
+            pltpu.VMEM((rows, columns), f32),
+            pltpu.VMEM((rows, columns), bf),
+            pltpu.VMEM((length, columns), f32),
+            pltpu.VMEM((rows, columns), f32),
+            pltpu.VMEM((rows // 2, columns), f32),
+            pltpu.VMEM((rows // 2, columns), bf),
+            pltpu.VMEM((rows // 2, columns), bf),
+            pltpu.VMEM((rows, columns), f32),
+            dma((steps, n)),
+            dma((steps, n)),
+            dma((steps, nz)),
+            dma((steps, nz)),
+            dma((steps, nz)),
+            dma((steps, nz)),
+            dma((steps, nz)),
+            dma((steps, nz)),
+            dma((steps, nz)),
+            dma((steps, nz)),
+            dma((3,)),
+            dma((3,)),
+        ],
+        compiler_params=pltpu.CompilerParams(collective_id=0, has_side_effects=True),
+    )(layer_input, queries, keys, targets, value_weight, outer_momentum)
+
+
 def solution(mesh):
     in_specs = (
         P(None, ("replica", "fsdp"), None),

time: 343 us -> 142 us (0.41)
  waiting for transfers between devices: 255 us -> 0 us
  Pallas kernels: 0 us -> 138 us
  matrix products: 30.8 us -> 0 us
  local copies, waits for them, and re-layouts: 27.2 us -> 3.32 us
  between operations: 13.9 us -> 0.65 us
  other arithmetic: 8.29 us -> 0 us
  starting transfers between devices: 7.66 us -> 0 us
    all_gather x4 -> x0, waiting for transfers between devices: 220 us -> none  [the longest x2 153 us: shards(): lax.all_gather(shard_bf, 'fsdp', axis=0, tiled=True)]
    pallas_call x0 -> x1, Pallas kernels: none -> 138 us  [shards(): pl.pallas_call(functools.partial(round_kernel, n), out_shape=(out, out),...]
    psum x1 -> x0, waiting for transfers between devices: 35.1 us -> none  [shards(): total_delta = lax.psum(value_weight - weights_now, 'replica')]
    dot_general x6 -> x0, matrix products: 23.8 us -> none  [the longest x2 8.66 us: shards(): jnp.einsum('gjqk,qgjd->kgd', attention, out_grad.reshape(length, KVH, gro...]
    unnamed x19 -> x4, local copies, waits for them, and re-layouts: 13.4 us -> 3.32 us
    all_to_all x1 -> x0, starting transfers between devices: 7.28 us -> none  [shards(): lax.all_to_all(layer_input, 'fsdp', split_axis=2, concat_axis=1, tiled=True)]
    slice x5 -> x0, local copies, waits for them, and re-layouts: 7.01 us -> none  [the longest x3 4.29 us: shards(): step_features = by_features[step_index]]
    sub x2 -> x0, matrix products: 6.95 us -> none  [shards(): expd = jnp.exp(scores - highest)]
  transfers between devices with their start and end apart: 6 -> 0, of which waited for: 5 -> 0; matrix products, arithmetic and copies ran while one was open for 12% -> 0% of each run, Pallas kernels for 0% -> 0%
where the time goes in v1:
time: 142 us
  Pallas kernels  138 us (97%)
  local copies, waits for them, and re-layouts  3.32 us (2%)
    pallas_call x1, Pallas kernels, shards(): pl.pallas_call(functools.partial(round_kernel, n), out_shape=(out, out),...  138 us
    unnamed x4, local copies, waits for them, and re-layouts  3.32 us

profile of v1, /device:TPU:0, one launch (start us, length us, event | category | flops | bytes accessed | tf_op | source)
XLA Modules:
  0.0 141.6 jit_solution(8638691241794464983)
XLA Ops:
  0.6 137.6 %shard_map.77 = (f32[512,512]{1,0:T(8,128)}, f32[512,512]{1,0:T(8,128)}) custom-call(bf16[2,128,4096]{2,1,0:T(8,128)(2,1)} %x_ref.1, bf16[2,128,4096]{2,1,0:T(8,128)(2,1)} %q_ref.1, bf16[2,128,512]{2,1,0:T(8,128)(2,1)} %k_ref.1, bf16[2,128,4096]{2,1,0:T(8,128)(2,1)} %t_ref.1, f32[512,512]{1,0:T(8,128)} %w_ref.1, f32[512,512]{1,0:T(8,128)} %om_ref.1), custom_call_target="tpu_custom_call" | custom-call | tf_op jit(solution)/shard_map/pallas_call | solution.py:427
  138.2 0.0 copy-start
  138.2 2.4 %copy.10 = f32[512,512]{1,0:T(8,128)} copy(f32[512,512]{1,0:T(8,128)} %get-tuple-element.4) | data formatting | bytes 2097152
  140.6 0.0 copy-done
  140.6 1.0 copy.11
Async XLA Ops:
  138.2 2.4 %copy-start = (f32[512,512]{1,0:T(8,128)S(1)}, f32[512,512]{1,0:T(8,128)}, u32[]{:S(2)}) copy-start(f32[512,512]{1,0:T(8,128)} %get-tuple-element.5) | copy-start | bytes 3145732

commit v2 on v1

--- a/solution.py
+++ b/solution.py
@@ -104,10 +104,12 @@
     k_ref,
     t_ref,
     w_ref,
-    om_ref,
-    nw_ref,
-    nm_ref,
+    mean_ref,
     feat,
+    q_buf,
+    k_buf,
+    t_buf,
+    w_buf,
     mat_hi,
     mat_lo,
     base,
@@ -139,9 +141,13 @@
     agx_r,
     rep_s,
     rep_r,
+    load_s,
 ):
     steps, length, _ = x_ref.shape
     rows, columns = w_ref.shape
+    parts = 2
+    width = columns // parts
+    wide = [slice(p * width, (p + 1) * width) for p in range(parts)]
     heads = columns // HD
     group = QH // KVH
     tok_rep = length * n
@@ -158,13 +164,27 @@
     def at(dz, dx):
         return ((z + dz + nz) % nz) * 2 + (px + dx) % 2
 
-    hops = [(dz, 1) for dz in range(nz)] + [(dz, 0) for dz in range(1, nz)]
+    def turn(i):
+        return (1 - core) * i + core * (nz - i) if i else 0
+
+    order = [*range(1, nz), 0]
+    hops = [(i, 1) for i in order] + [(i, 0) for i in range(1, nz)]
+
+    loads = {}
+
+    def load(i, src, dst):
+        loads[i] = pltpu.make_async_copy(src, dst, load_s.at[i])
+        loads[i].start()
 
     barrier = pltpu.get_barrier_semaphore()
     for dz, dx in hops:
         pl.semaphore_signal(barrier, inc=1, device_id={"fsdp": at(dz, dx)}, device_id_type=MESH)
     for peer in (core_peer, pair_peer):
         pl.semaphore_signal(barrier, inc=1, device_id={"replica": peer}, device_id_type=MESH)
+    load(steps, q_ref, q_buf)
+    load(steps + 1, k_ref, k_buf)
+    load(steps + 2, t_ref, t_buf)
+    load(steps + 3, w_ref, w_buf)
     pl.semaphore_wait(barrier, n + 1)
 
     def send(src, dst, ssem, rsem, axis, peer):
@@ -179,12 +199,13 @@
         copy.start()
         return copy
 
-    def send_inputs(s):
+    def send_inputs(s, only=None):
         copies = {}
-        for dz, dx in hops:
+        for k, dx in only or hops:
+            dz = turn(k)
             peer = at(dz, dx)
             i = dz * 2 + dx
-            copies[dz, dx] = send(
+            copies[k, dx] = send(
                 x_ref.at[s, :, pl.ds(pl.multiple_of(peer * rows, 128), rows)],
                 feat.at[s, me],
                 in_s.at[s, i],
@@ -200,12 +221,12 @@
 
     def attention_of(s):
         def one(g, carry):
-            keys = k_ref[s, :, pl.ds(pl.multiple_of(g * HD, HD), HD)]
+            keys = k_buf[s, :, pl.ds(pl.multiple_of(g * HD, HD), HD)]
             both = jnp.zeros((length, length + HD), jnp.float32)
             for j in range(group):
                 cols = pl.ds(pl.multiple_of((g * group + j) * HD, HD), HD)
                 scores = lax.dot_general(
-                    q_ref[s, :, cols],
+                    q_buf[s, :, cols],
                     keys,
                     (((1,), (1,)), ((), ())),
                     preferred_element_type=jnp.float32,
@@ -216,7 +237,7 @@
                 att = (expd / jnp.sum(expd, axis=-1, keepdims=True)).astype(jnp.bfloat16)
                 both += lax.dot_general(
                     att,
-                    jnp.concatenate([att, t_ref[s, :, cols]], axis=1),
+                    jnp.concatenate([att, t_buf[s, :, cols]], axis=1),
                     (((0,), (0,)), ((), ())),
                     preferred_element_type=jnp.float32,
                 )
@@ -241,122 +262,118 @@
     pending = []
     inputs = {0: send_inputs(0)}
     for s in range(steps):
-        feat[s, me] = x_ref[s, :, pl.ds(pl.multiple_of(me * rows, 128), rows)]
+        load(
+            s,
+            x_ref.at[s, :, pl.ds(pl.multiple_of(me * rows, 128), rows)],
+            feat.at[s, me],
+        )
 
     def cast_weights(c):
-        wbf[c, :] = w_ref[c, :].astype(jnp.bfloat16)
-
+        wbf[c, :] = w_buf[c, :].astype(jnp.bfloat16)
+
+    loads[steps + 3].wait()
     chunks(cast_weights)
+    for i in (*range(steps), steps, steps + 1, steps + 2):
+        loads[i].wait()
     for s in range(steps):
         attention_of(s)
 
     for s in range(steps):
-        def partial(j):
-            return jnp.dot(feat[s, j], wbf[...], preferred_element_type=jnp.float32)
-
-        def wait_input(dz, dx):
-            inputs[s][(nz - dz) % nz, dx].wait_recv()
-
-        sides = []
-        for dz in range(nz):
-            wait_input(dz, 1)
-            side_out[s, dz] = partial(at(dz, 1)).astype(jnp.bfloat16)
-            sides.append(
-                send(
-                    side_out.at[s, dz],
-                    side_in.at[s, dz],
-                    side_s.at[s, dz],
-                    side_r.at[s, dz],
+        def partial(j, p):
+            return jnp.dot(feat[s, j], wbf[:, wide[p]], preferred_element_type=jnp.float32)
+
+        if s + 1 < steps:
+            inputs[s + 1] = send_inputs(s + 1, hops[:2])
+        sides = {}
+        for k in order:
+            inputs[s][k, 1].wait_recv()
+            dz = (nz - turn(k)) % nz if k else 0
+            for p in range(parts):
+                side_out[s, dz, :, wide[p]] = partial(at(dz, 1), p).astype(jnp.bfloat16)
+                sides[k, p] = send(
+                    side_out.at[s, dz, :, wide[p]],
+                    side_in.at[s, dz, :, wide[p]],
+                    side_s.at[s, dz, p],
+                    side_r.at[s, dz, p],
                     "fsdp",
                     side,
                 )
-            )
-        cols = []
-        for dz in list(range(1, nz)) + [0]:
-            if dz:
-                wait_input(dz, 0)
-            own = partial(at(dz, 0))
-            sides[dz].wait_recv()
-            own = own + side_in[s, dz].astype(jnp.float32)
-            if dz:
-                col_out[s, dz] = own.astype(jnp.bfloat16)
-                cols.append(
-                    send(
-                        col_out.at[s, dz],
-                        col_in.at[s, dz],
-                        col_s.at[s, dz],
-                        col_r.at[s, dz],
+        cols = {}
+        for k in order:
+            dz = (nz - turn(k)) % nz if k else 0
+            if k:
+                inputs[s][k, 0].wait_recv()
+            for p in range(parts):
+                own = partial(at(dz, 0), p)
+                sides[k, p].wait_recv()
+                own = own + side_in[s, dz, :, wide[p]].astype(jnp.float32)
+                if k:
+                    col_out[s, dz, :, wide[p]] = own.astype(jnp.bfloat16)
+                    cols[k, p] = send(
+                        col_out.at[s, dz, :, wide[p]],
+                        col_in.at[s, dz, :, wide[p]],
+                        col_s.at[s, dz, p],
+                        col_r.at[s, dz, p],
                         "fsdp",
                         at(dz, 0),
                     )
-                )
-            else:
-                acc[...] = own
-        if s + 1 < steps:
-            inputs[s + 1] = send_inputs(s + 1)
-        for dz in range(1, nz):
-            cols[dz - 1].wait_recv()
-        pending += sides + cols + list(inputs[s].values())
-
-        summed = acc[...]
-        for dz in range(1, nz):
-            summed = summed + col_in[s, dz].astype(jnp.float32)
-        values = (summed / math.sqrt(D)).astype(jnp.bfloat16)
-        for g in range(heads):
-            part = values[:, g * HD : (g + 1) * HD]
-            vg = jnp.dot(mat_hi[s, g], part, preferred_element_type=jnp.float32)
-            vg += jnp.dot(mat_lo[s, g], part, preferred_element_type=jnp.float32)
-            vg = (vg - base[s, g]) / tok_rep
-            vgrad[s, me, :, g * HD : (g + 1) * HD] = vg.astype(jnp.bfloat16)
-
-        def add_block(j, first=False):
+                else:
+                    acc[:, wide[p]] = own
+        pending += [*sides.values(), *cols.values(), *inputs[s].values()]
+
+        def add_block(j, p, first=False):
             term = lax.dot_general(
                 feat[s, j],
-                vgrad[s, j],
+                vgrad[s, j, :, wide[p]],
                 (((0,), (0,)), ((), ())),
                 preferred_element_type=jnp.float32,
             )
             if first:
-                grad[...] = term
+                grad[:, wide[p]] = term
             else:
-                grad[...] += term
-
-        zs = []
-        for dz in range(1, nz):
-            zs.append(
-                send(
-                    vgrad.at[s, me],
-                    vgrad.at[s, me],
-                    agz_s.at[s, dz],
-                    agz_r.at[s, dz],
-                    "fsdp",
-                    at(dz, 0),
+                grad[:, wide[p]] += term
+
+        def forward(j, i, p):
+            block = vgrad.at[s, j, :, wide[p]]
+            return send(block, block, agx_s.at[s, i, p], agx_r.at[s, i, p], "fsdp", side)
+
+        zs = {}
+        xs = {}
+        for p in range(parts):
+            summed = acc[:, wide[p]]
+            for k in range(1, nz):
+                cols[k, p].wait_recv()
+            for dz in range(1, nz):
+                summed = summed + col_in[s, dz, :, wide[p]].astype(jnp.float32)
+            values = (summed / math.sqrt(D)).astype(jnp.bfloat16)
+            for i in range(width // HD):
+                g = p * (width // HD) + i
+                part = values[:, i * HD : (i + 1) * HD]
+                vg = jnp.dot(mat_hi[s, g], part, preferred_element_type=jnp.float32)
+                vg += jnp.dot(mat_lo[s, g], part, preferred_element_type=jnp.float32)
+                vg = (vg - base[s, g]) / tok_rep
+                vgrad[s, me, :, g * HD : (g + 1) * HD] = vg.astype(jnp.bfloat16)
+            block = vgrad.at[s, me, :, wide[p]]
+            for k in range(1, nz):
+                dz = turn(k)
+                zs[k, p] = send(
+                    block, block, agz_s.at[s, dz, p], agz_r.at[s, dz, p], "fsdp", at(dz, 0)
                 )
-            )
-        xs = [
-            send(
-                vgrad.at[s, me], vgrad.at[s, me], agx_s.at[s, 0], agx_r.at[s, 0], "fsdp", side
-            )
-        ]
-        add_block(me, True)
-        for dz in (1, *range(nz - 1, 1, -1)):
-            j = at(-dz, 0)
-            zs[dz - 1].wait_recv()
-            xs.append(
-                send(
-                    vgrad.at[s, j],
-                    vgrad.at[s, j],
-                    agx_s.at[s, dz],
-                    agx_r.at[s, dz],
-                    "fsdp",
-                    side,
-                )
-            )
-            add_block(j)
-        for i, dz in enumerate((0, 1, *range(nz - 1, 1, -1))):
-            xs[i].wait_recv()
-            add_block(at(-dz, 1))
-        pending += zs + xs
+            xs[0, p] = forward(me, 0, p)
+        for p in range(parts):
+            add_block(me, p, True)
+        for p in range(parts):
+            for k in range(1, nz):
+                zs[k, p].wait_recv()
+                xs[k, p] = forward(at(-turn(k), 0), turn(k), p)
+                add_block(at(-turn(k), 0), p)
+        if s + 1 < steps:
+            inputs[s + 1].update(send_inputs(s + 1, hops[2:]))
+        for p in range(parts):
+            for k in range(nz):
+                xs[k, p].wait_recv()
+                add_block(at(-turn(k), 1), p)
+        pending += [*zs.values(), *xs.values()]
 
         def adam(c):
             gradient = grad[c, :] / math.sqrt(D)
@@ -365,7 +382,7 @@
             if s:
                 one = beta_one * mom_one[c, :] + one
                 two = beta_two * mom_two[c, :] + two
-            now = theta[c, :] if s else w_ref[c, :]
+            now = theta[c, :] if s else w_buf[c, :]
             fixed_one = one / (1.0 - beta_one ** (s + 1))
             fixed_two = two / (1.0 - beta_two ** (s + 1))
             now = now - inner_rate * (
@@ -377,38 +394,80 @@
                 theta[c, :] = now
                 wbf[c, :] = now.astype(jnp.bfloat16)
             else:
-                delta[c, :] = w_ref[c, :] - now
-
-        chunks(adam)
+                delta[c, :] = w_buf[c, :] - now
+
+        if s + 1 < steps:
+            chunks(adam)
 
     half = rows // 2
-    mine = pl.ds(pl.multiple_of(core * half, 128), half)
-    other = pl.ds(pl.multiple_of((1 - core) * half, 128), half)
-    first = send(delta.at[other], core_in, rep_s.at[0], rep_r.at[0], "replica", core_peer)
-    first.wait_recv()
-    pair_out[...] = (delta[mine, :] + core_in[...]).astype(jnp.bfloat16)
-    second = send(pair_out, pair_in, rep_s.at[1], rep_r.at[1], "replica", pair_peer)
-    second.wait_recv()
-    total[mine, :] = pair_out[...].astype(jnp.float32) + pair_in[...].astype(jnp.float32)
-    third = send(
-        total.at[mine], total.at[mine], rep_s.at[2], rep_r.at[2], "replica", core_peer
-    )
-
-    def finish(start):
+    piece = half // parts
+
+    def span(which, p):
+        return pl.multiple_of(which * half + p * piece, 128)
+
+    def over(start, body):
         def step(i, carry):
-            c = pl.ds(pl.multiple_of(start + i * chunk, chunk), chunk)
-            mean = total[c, :] / 4
-            momentum = outer_mu * om_ref[c, :] + mean
-            nm_ref[c, :] = momentum
-            nw_ref[c, :] = w_ref[c, :] - outer_rate * (mean + outer_mu * momentum)
+            body(pl.ds(pl.multiple_of(start + i * chunk, chunk), chunk))
             return carry
 
-        lax.fori_loop(0, half // chunk, step, 0)
-
-    finish(core * half)
-    third.wait_recv()
-    finish((1 - core) * half)
-    for copy in pending + [first, second, third]:
+        lax.fori_loop(0, piece // chunk, step, 0)
+
+    first, second, third = [], [], []
+    for p in range(parts):
+        over(span(1 - core, p), adam)
+        first.append(
+            send(
+                delta.at[pl.ds(span(1 - core, p), piece)],
+                core_in.at[pl.ds(p * piece, piece)],
+                rep_s.at[0, p],
+                rep_r.at[0, p],
+                "replica",
+                core_peer,
+            )
+        )
+    for p in range(parts):
+        over(span(core, p), adam)
+        first[p].wait_recv()
+        rows_p = pl.ds(p * piece, piece)
+        pair_out[rows_p, :] = (
+            delta[pl.ds(span(core, p), piece), :] + core_in[rows_p, :]
+        ).astype(jnp.bfloat16)
+        second.append(
+            send(
+                pair_out.at[rows_p],
+                pair_in.at[rows_p],
+                rep_s.at[1, p],
+                rep_r.at[1, p],
+                "replica",
+                pair_peer,
+            )
+        )
+
+    def finish(c):
+        mean_ref[c, :] = total[c, :] / 4
+
+    for p in range(parts):
+        second[p].wait_recv()
+        rows_p = pl.ds(p * piece, piece)
+        mine = pl.ds(span(core, p), piece)
+        total[mine, :] = pair_out[rows_p, :].astype(jnp.float32) + pair_in[
+            rows_p, :
+        ].astype(jnp.float32)
+        third.append(
+            send(
+                total.at[mine],
+                total.at[mine],
+                rep_s.at[2, p],
+                rep_r.at[2, p],
+                "replica",
+                core_peer,
+            )
+        )
+        over(span(core, p), finish)
+    for p in range(parts):
+        third[p].wait_recv()
+        over(span(1 - core, p), finish)
+    for copy in pending + first + second + third:
         copy.wait_send()
 
 
@@ -417,20 +476,24 @@
     replicas = lax.axis_size("replica")
     rows, columns = value_weight.shape
     steps, length, _ = layer_input.shape
-    if rows % 256 or n % 2 or replicas != 4 or length % 128:
+    if rows % 512 or columns % (2 * HD) or n % 2 or replicas != 4 or length % 128:
         return plain_shards(layer_input, queries, keys, targets, value_weight, outer_momentum)
     nz = n // 2
     heads = columns // HD
     bf, f32 = jnp.bfloat16, jnp.float32
     dma = pltpu.SemaphoreType.DMA
     out = jax.ShapeDtypeStruct((rows, columns), f32)
-    return pl.pallas_call(
+    mean_delta = pl.pallas_call(
         functools.partial(round_kernel, n),
-        out_shape=(out, out),
-        in_specs=[pl.BlockSpec(memory_space=pltpu.VMEM)] * 6,
-        out_specs=(pl.BlockSpec(memory_space=pltpu.VMEM),) * 2,
+        out_shape=out,
+        in_specs=[pl.BlockSpec(memory_space=pl.ANY)] * 5,
+        out_specs=pl.BlockSpec(memory_space=pltpu.VMEM),
         scratch_shapes=[
             pltpu.VMEM((steps, n, length, rows), bf),
+            pltpu.VMEM(queries.shape, bf),
+            pltpu.VMEM(keys.shape, bf),
+            pltpu.VMEM(targets.shape, bf),
+            pltpu.VMEM((rows, columns), f32),
             pltpu.VMEM((steps, heads, length, length), bf),
             pltpu.VMEM((steps, heads, length, length), bf),
             pltpu.VMEM((steps, heads, length, HD), f32),
@@ -452,19 +515,23 @@
             pltpu.VMEM((rows, columns), f32),
             dma((steps, n)),
             dma((steps, n)),
-            dma((steps, nz)),
-            dma((steps, nz)),
-            dma((steps, nz)),
-            dma((steps, nz)),
-            dma((steps, nz)),
-            dma((steps, nz)),
-            dma((steps, nz)),
-            dma((steps, nz)),
-            dma((3,)),
-            dma((3,)),
+            dma((steps, nz, 2)),
+            dma((steps, nz, 2)),
+            dma((steps, nz, 2)),
+            dma((steps, nz, 2)),
+            dma((steps, nz, 2)),
+            dma((steps, nz, 2)),
+            dma((steps, nz, 2)),
+            dma((steps, nz, 2)),
+            dma((3, 2)),
+            dma((3, 2)),
+            dma((steps + 4,)),
         ],
         compiler_params=pltpu.CompilerParams(collective_id=0, has_side_effects=True),
-    )(layer_input, queries, keys, targets, value_weight, outer_momentum)
+    )(layer_input, queries, keys, targets, value_weight)
+    new_momentum = outer_mu * outer_momentum + mean_delta
+    new_weight = value_weight - outer_rate * (mean_delta + outer_mu * new_momentum)
+    return (new_weight, new_momentum)
 
 
 def solution(mesh):

time: 142 us -> 120 us (0.85)
  Pallas kernels: 138 us -> 116 us
  local copies, waits for them, and re-layouts: 3.32 us -> 0.01 us
  other arithmetic: 0 us -> 2.93 us
    pallas_call x1, Pallas kernels: 138 us -> 116 us  [shards(): pl.pallas_call(functools.partial(round_kernel, n), out_shape=out, in_spec...]
    unnamed x4, local copies, waits for them, and re-layouts: 3.32 us -> 0.01 us
    sub x0 -> x1, other arithmetic: none -> 2.93 us  [shards(): value_weight - outer_rate * (mean_delta + outer_mu * new_momentum)]
where the time goes in v2:
time: 120 us
  Pallas kernels  116 us (97%)
  other arithmetic  2.93 us (2%)
    pallas_call x1, Pallas kernels, shards(): pl.pallas_call(functools.partial(round_kernel, n), out_shape=out, in_spec...  116 us
    sub x1, other arithmetic, shards(): value_weight - outer_rate * (mean_delta + outer_mu * new_momentum)  2.93 us

profile of v2, /device:TPU:0, one launch (start us, length us, event | category | flops | bytes accessed | tf_op | source)
XLA Modules:
  0.0 119.7 jit_solution(16036313221647872617)
XLA Ops:
  0.6 0.0 copy-start
  0.6 0.0 copy-start.1
  0.7 116.0 %shard_map.77 = f32[512,512]{1,0:T(8,128)} custom-call(bf16[2,128,4096]{2,1,0:T(8,128)(2,1)} %x_ref.1, bf16[2,128,4096]{2,1,0:T(8,128)(2,1)} %q_ref.1, bf16[2,128,512]{2,1,0:T(8,128)(2,1)} %k_ref.1, bf16[2,128,4096]{2,1,0:T(8,128)(2,1)} %t_ref.1, f32[512,512]{1,0:T(8,128)} %w_ref.1), custom_call_target="tpu_custom_call" | custom-call | tf_op jit(solution)/shard_map/pallas_call | solution.py:486
  116.7 0.0 copy-done
  116.7 0.0 copy-done.1
  116.7 2.9 %multiply_subtract_fusion = (f32[512,512]{1,0:T(8,128)}, f32[512,512]{1,0:T(8,128)}) fusion(f32[512,512]{1,0:T(8,128)S(1)} %copy-done, f32[512,512]{1,0:T(8,128)} %shard_map.77, f32[512,512]{1,0:T(8,128)S(1)} %copy-done.1), kind=kLoop, calls=%fused_computation | loop fusion | flops 1572864 | bytes 5242880 | tf_op jit(solution)/shard_map/sub | solution.py:533
Async XLA Ops:
  0.6 116.1 %copy-start = (f32[512,512]{1,0:T(8,128)S(1)}, f32[512,512]{1,0:T(8,128)}, u32[]{:S(2)}) copy-start(f32[512,512]{1,0:T(8,128)} %w_ref.1) | copy-start | bytes 3145732
  0.6 116.1 %copy-start.1 = (f32[512,512]{1,0:T(8,128)S(1)}, f32[512,512]{1,0:T(8,128)}, u32[]{:S(2)}) copy-start(f32[512,512]{1,0:T(8,128)} %param.11) | copy-start | bytes 3145732
